TPU v7x, 32 devices: a whole 2x2x4 slice. The times are simulated.
32 devices in a mesh: sx: 8 (over z, y), sy: 4 (over x, core).
Axes of the slice: x: 2, y: 2, z: 4, core: 2. Of those that a mesh axis runs over, the one named last changes fastest.
Arguments:
- tensors: bfloat16 [2, 8, 4, 1024, 256], P(None, 'sx', 'sy'), may hold values from -6 to 6
- gates: bfloat16 [5, 2, 2, 256, 256], replicated, may hold values from -0.1875 to 0.1875
- closing_rows: bfloat16 [2, 4096, 1024], P(None, ('sx', 'sy')), may hold values from -0.125 to 0.125
- closing_columns: float32 [2, 4096, 256], P(None, ('sx', 'sy')), may hold values from -0.25 to 0.25
Outputs:
- amplitudes: float32 [2, 4096], replicated
All inputs are finite; a program needn't handle non-finite values.
Results may differ from a plain program's by a relative error of at most 0.012.
Values may be sent and summed in bfloat16 or wider, within the bound.
A program may use at most 64 MiB of HBM per device.

v0:
```python
import jax
import jax.numpy as jnp
from jax import lax
from jax.sharding import PartitionSpec as P


def mixing_matrix(gate_pair, sign):
    own_top = jnp.concatenate([gate_pair[0, 0], gate_pair[0, 1]], axis=1)
    own_low = jnp.concatenate([-gate_pair[0, 1], gate_pair[0, 0]], axis=1)
    far_top = jnp.concatenate([gate_pair[1, 0], gate_pair[1, 1]], axis=1) * sign
    far_low = jnp.concatenate([-gate_pair[1, 1], gate_pair[1, 0]], axis=1) * sign
    return jnp.concatenate([own_top, own_low, far_top, far_low], axis=0)


def combine(own, partner, matrix):
    width = own.shape[-1]
    leading = own.shape[1:-1]
    joined = jnp.concatenate([own[0], own[1], partner[0], partner[1]], axis=-1).reshape(
        -1, 4 * width
    )
    result = jnp.dot(joined, matrix, preferred_element_type=jnp.float32).astype(jnp.bfloat16)
    real_part = result[:, :width].reshape(leading + (width,))
    imag_part = result[:, width:].reshape(leading + (width,))
    return jnp.stack([real_part, imag_part])


def local_section(grouped, gate_pair, axis_dim, bit_pos):
    shape = grouped.shape
    count = shape[axis_dim]
    split = shape[:axis_dim] + (count >> bit_pos + 1, 2, 1 << bit_pos) + shape[axis_dim + 1 :]
    blocks = grouped.reshape(split)
    lower = lax.index_in_dim(blocks, 0, axis_dim + 1, keepdims=False)
    upper = lax.index_in_dim(blocks, 1, axis_dim + 1, keepdims=False)
    new_lower = combine(lower, upper, mixing_matrix(gate_pair, 1.0))
    new_upper = combine(upper, lower, mixing_matrix(gate_pair, -1.0))
    return jnp.stack([new_lower, new_upper], axis=axis_dim + 1).reshape(shape)


def close_columns(projected, closing_columns):
    amp_real = jnp.sum(
        projected[0] * closing_columns[0] - projected[1] * closing_columns[1], axis=-1
    )
    amp_imag = jnp.sum(
        projected[0] * closing_columns[1] + projected[1] * closing_columns[0], axis=-1
    )
    return jnp.stack([amp_real, amp_imag])


def combine_rows(closing_rows, current):
    proj_real = jnp.dot(closing_rows[0], current[0], preferred_element_type=jnp.float32) - jnp.dot(
        closing_rows[1], current[1], preferred_element_type=jnp.float32
    )
    proj_imag = jnp.dot(closing_rows[0], current[1], preferred_element_type=jnp.float32) + jnp.dot(
        closing_rows[1], current[0], preferred_element_type=jnp.float32
    )
    return jnp.stack([proj_real, proj_imag])


def local(tensors, gates, closing_rows, closing_columns):
    current = tensors[:, 0, 0]
    rows_dev = current.shape[1]
    width = current.shape[2]
    count_x = lax.axis_size("sx")
    count_y = lax.axis_size("sy")
    bits_x = count_x.bit_length() - 1
    bits_y = count_y.bit_length() - 1
    grouped = lax.all_to_all(
        current.reshape(2, count_x, rows_dev // count_x, width),
        "sx",
        split_axis=1,
        concat_axis=1,
        tiled=True,
    )
    for bit_pos in range(bits_x):
        grouped = local_section(grouped, gates[bit_pos], 1, bit_pos)
    current = lax.all_to_all(grouped, "sx", split_axis=1, concat_axis=1, tiled=True).reshape(
        2, rows_dev, width
    )
    grouped = lax.all_to_all(
        current.reshape(2, count_y, rows_dev // count_y, width),
        "sy",
        split_axis=1,
        concat_axis=1,
        tiled=True,
    )
    for bit_pos in range(bits_y):
        grouped = local_section(grouped, gates[bits_x + bit_pos], 1, bit_pos)
    current = lax.all_to_all(grouped, "sy", split_axis=1, concat_axis=1, tiled=True).reshape(
        2, rows_dev, width
    )
    closed = close_columns(combine_rows(closing_rows, current), closing_columns)
    return lax.all_gather(closed, ("sx", "sy"), axis=1, tiled=True)


def solution(mesh):
    placed = (
        P(None, "sx", "sy", None, None),
        P(),
        P(None, ("sx", "sy"), None),
        P(None, ("sx", "sy"), None),
    )
    return jax.shard_map(local, mesh=mesh, in_specs=placed, out_specs=P(), check_vma=False)
```

profile of v0, /device:TPU:0, one launch (start us, length us, event | category | flops | bytes accessed | tf_op | source)
XLA Modules:
  0.0 157.4 jit_solution(10815839486201930402)
XLA Ops:
  0.0 2.3 %copy.47 = bf16[2,8,128,256]{3,2,0,1:T(8,128)(2,1)} copy(bf16[2,8,128,256]{3,2,1,0:T(8,128)(2,1)} %bitcast.207) | data formatting | bytes 2097152 | tf_op jit(solution)/shard_map/reshape;squeeze | solution.py:68
  2.3 7.3 %all-to-all-start = ((bf16[2,8,128,256]{3,2,0,1:T(8,128)(2,1)}), bf16[2,8,128,256]{3,2,0,1:T(8,128)(2,1)S(1)}, u32[]{:S(2)}, u32[]{:S(2)}) async-start(bf16[2,8,128,256]{3,2,0,1:T(8,128)(2,1)} %copy.47), calls=%async_computation | async-start | bytes 2097152 | tf_op jit(solution)/shard_map/all_to_all | solution.py:67
  9.6 1.9 %slice_bitcast_fusion = (bf16[2,2,256,256]{3,2,1,0:T(8,128)(2,1)S(1)}, bf16[2,2,256,256]{3,2,1,0:T(8,128)(2,1)S(1)}, bf16[2,2,256,256]{3,2,1,0:T(8,128)(2,1)S(1)...) fusion(bf16[5,2,2,256,256]{4,3,2,1,0:T(8,128)(2,1)} %param.5), kind=kLoop, calls=%fused_computation.162 | loop fusion | bytes 5242880 | tf_op jit(solution)/shard_map/squeeze | solution.py:87
  11.5 0.7 slice_bitcast_fusion.23
  12.2 0.7 fusion.156
  13.0 0.9 maximum_multiply_fusion
  13.9 0.8 slice_bitcast_fusion.15
  14.7 0.9 maximum_multiply_fusion.2
  15.6 0.8 fusion.160
  16.3 0.9 maximum_multiply_fusion.4
  17.2 18.2 %all-to-all-done = bf16[2,8,128,256]{3,2,0,1:T(8,128)(2,1)S(1)} async-done(((bf16[2,8,128,256]{3,2,0,1:T(8,128)(2,1)}), bf16[2,8,128,256]{3,2,0,1:T(8,128)(2,1)S(1)}, u32[]{:S(2)}, u32[]{:S(2)}) %all-to-all-start) | async-done | bytes 1048608 | tf_op jit(solution)/shard_map/all_to_all | solution.py:67
  35.5 0.8 copy-done.23
  39.4 0.7 convolution_convert_fusion.7
  44.5 29.3 %all_to_all.20 = bf16[2,8,128,256]{3,2,0,1:T(8,128)(2,1)S(1)} all-to-all(bf16[2,8,128,256]{3,2,0,1:T(8,128)(2,1)S(1)} %copy.56), channel_id=1, replica_groups=mesh['sx'=8,'sy'=4] {'sx'}, dimensions={1} | all-to-all | bytes 2097152 | tf_op jit(solution)/shard_map/all_to_all | solution.py:76
  73.9 1.1 copy.58
  75.0 3.5 %all-to-all-start.2 = ((bf16[2,4,256,256]{3,2,0,1:T(8,128)(2,1)}), bf16[2,4,256,256]{3,2,0,1:T(8,128)(2,1)S(1)}, u32[]{:S(2)}, u32[]{:S(2)}) async-start(bf16[2,4,256,256]{3,2,0,1:T(8,128)(2,1)} %copy.58), calls=%async_computation.2 | async-start | bytes 2097152 | tf_op jit(solution)/shard_map/all_to_all | solution.py:79
  78.5 0.8 slice_bitcast_fusion.7
  79.3 0.9 maximum_multiply_fusion.6
  80.9 12.0 %all-to-all-done.2 = bf16[2,4,256,256]{3,2,0,1:T(8,128)(2,1)S(1)} async-done(((bf16[2,4,256,256]{3,2,0,1:T(8,128)(2,1)}), bf16[2,4,256,256]{3,2,0,1:T(8,128)(2,1)S(1)}, u32[]{:S(2)}, u32[]{:S(2)}) %all-to-all-start.2) | async-done | bytes 1048608 | tf_op jit(solution)/shard_map/all_to_all | solution.py:79
  93.0 0.7 convolution_convert_fusion.3
  97.8 1.1 copy.65
  98.9 3.5 %all-to-all-start.3 = ((bf16[2,4,256,256]{3,2,0,1:T(8,128)(2,1)}), bf16[2,4,256,256]{3,2,0,1:T(8,128)(2,1)S(1)}, u32[]{:S(2)}, u32[]{:S(2)}) async-start(bf16[2,4,256,256]{3,2,0,1:T(8,128)(2,1)} %copy.65), calls=%async_computation.3 | async-start | bytes 2097152 | tf_op jit(solution)/shard_map/all_to_all | solution.py:88
  102.6 14.2 %all-to-all-done.3 = bf16[2,4,256,256]{3,2,0,1:T(8,128)(2,1)S(1)} async-done(((bf16[2,4,256,256]{3,2,0,1:T(8,128)(2,1)}), bf16[2,4,256,256]{3,2,0,1:T(8,128)(2,1)S(1)}, u32[]{:S(2)}, u32[]{:S(2)}) %all-to-all-start.3) | async-done | bytes 1048608 | tf_op jit(solution)/shard_map/all_to_all | solution.py:88
  118.3 38.6 %all_gather.3 = f32[2,4096]{1,0:T(2,128)S(1)} all-gather(f32[2,128]{1,0:T(2,128)S(1)} %pad_maximum_fusion.3), channel_id=1, replica_groups=mesh['sx'=8,'sy'=4] {'sx','sy'}, dimensions={1}, use_global_device_ids=true | all-gather | bytes 33792 | tf_op jit(solution)/shard_map/all_gather | solution.py:92
  (105 shorter events, 14.4 us)
Async XLA Ops:
  2.3 33.1 %all-to-all-start = ((bf16[2,8,128,256]{3,2,0,1:T(8,128)(2,1)}), bf16[2,8,128,256]{3,2,0,1:T(8,128)(2,1)S(1)}, u32[]{:S(2)}, u32[]{:S(2)}) async-start(bf16[2,8,128,256]{3,2,0,1:T(8,128)(2,1)} %copy.47), calls=%async_computation | async-start | bytes 2097152 | tf_op jit(solution)/shard_map/all_to_all | solution.py:67
  35.4 1.0 copy-start.24
  35.4 1.0 copy-start.25
  36.4 0.9 copy-start.5
  36.4 1.0 copy-start.6
  38.4 1.0 copy-start.12
  38.4 1.0 copy-start.22
  39.4 0.9 copy-start.3
  39.4 1.0 copy-start.4
  41.4 1.0 copy-start.21
  42.3 1.0 copy-start.2
  75.0 17.9 %all-to-all-start.2 = ((bf16[2,4,256,256]{3,2,0,1:T(8,128)(2,1)}), bf16[2,4,256,256]{3,2,0,1:T(8,128)(2,1)S(1)}, u32[]{:S(2)}, u32[]{:S(2)}) async-start(bf16[2,4,256,256]{3,2,0,1:T(8,128)(2,1)} %copy.58), calls=%async_computation.2 | async-start | bytes 2097152 | tf_op jit(solution)/shard_map/all_to_all | solution.py:79
  79.2 13.7 %copy-start.14 = (bf16[256,256]{1,0:T(8,128)(2,1)S(1)}, bf16[256,256]{1,0:T(8,128)(2,1)}, u32[]{:S(2)}) copy-start(bf16[256,256]{1,0:T(8,128)(2,1)} %get-tuple-element.96) | copy-start | bytes 393220
  79.2 13.7 %copy-start.16 = (bf16[256,256]{1,0:T(8,128)(2,1)S(1)}, bf16[256,256]{1,0:T(8,128)(2,1)}, u32[]{:S(2)}) copy-start(bf16[256,256]{1,0:T(8,128)(2,1)} %get-tuple-element.99) | copy-start | bytes 393220
  79.2 13.7 %copy-start.19 = (bf16[256,256]{1,0:T(8,128)(2,1)S(1)}, bf16[256,256]{1,0:T(8,128)(2,1)}, u32[]{:S(2)}) copy-start(bf16[256,256]{1,0:T(8,128)(2,1)} %get-tuple-element.107) | copy-start | bytes 393220
  93.0 1.0 copy-start.7
  93.0 1.0 copy-start.8
  93.0 1.0 copy-start.15
  93.0 1.1 copy-start.17
  93.0 1.1 copy-start.20
  95.1 1.0 copy-start.18
  97.8 4.6 %copy-start.9 = (f32[2,128,256]{2,1,0:T(8,128)S(1)}, f32[2,128,256]{2,1,0:T(8,128)}, u32[]{:S(2)}) copy-start(f32[2,128,256]{2,1,0:T(8,128)} %param.7) | copy-start | bytes 786436
  98.9 17.9 %all-to-all-start.3 = ((bf16[2,4,256,256]{3,2,0,1:T(8,128)(2,1)}), bf16[2,4,256,256]{3,2,0,1:T(8,128)(2,1)S(1)}, u32[]{:S(2)}, u32[]{:S(2)}) async-start(bf16[2,4,256,256]{3,2,0,1:T(8,128)(2,1)} %copy.65), calls=%async_computation.3 | async-start | bytes 2097152 | tf_op jit(solution)/shard_map/all_to_all | solution.py:88
  102.4 14.5 %copy-start = (bf16[2,128,1024]{2,1,0:T(8,128)(2,1)S(1)}, bf16[2,128,1024]{2,1,0:T(8,128)(2,1)}, u32[]{:S(2)}) copy-start(bf16[2,128,1024]{2,1,0:T(8,128)(2,1)} %param.6) | copy-start | bytes 1572868
  (5 other events, 4.6 us)
where the time goes:
time: 158 us; the launch traced here: 157 us
  blocking collectives  67.9 us (43%)
  waiting for transfers between devices  44.3 us (28%)
  local copies, waits for them, and re-layouts  15.1 us (10%)
  starting transfers between devices  14.3 us (9%)
  matrix products  8.46 us (5%)
  other arithmetic  6.72 us (4%)
    all_gather x1, blocking collectives, local(): return lax.all_gather(closed, ('sx', 'sy'), axis=1, tiled=True)  38.6 us
    all_to_all x1, blocking collectives, local(): lax.all_to_all(grouped, 'sx', split_axis=1, concat_axis=1, tiled=True)  29.3 us
    all_to_all x1, waiting for transfers between devices, local(): lax.all_to_all(current.reshape(2, count_x, rows_dev // count_x, width), '...  18.2 us
    all_to_all x1, waiting for transfers between devices, local(): lax.all_to_all(grouped, 'sy', split_axis=1, concat_axis=1, tiled=True)  14.2 us
    all_to_all x1, waiting for transfers between devices, local(): lax.all_to_all(current.reshape(2, count_y, rows_dev // count_y, width), '...  12 us
    all_to_all x1, starting transfers between devices, local(): lax.all_to_all(current.reshape(2, count_x, rows_dev // count_x, width), '...  7.31 us
    dot_general x10, matrix products, combine(): jnp.dot(joined, matrix, preferred_element_type=jnp.float32)  7.1 us
    unnamed x59, local copies, waits for them, and re-layouts  5.51 us
  transfers between devices with their start and end apart: 3, of which 3 were waited for; matrix products, arithmetic and copies ran while one was open for 6% of the time, Pallas kernels for 0%

commit v1 on v0

--- a/solution.py
+++ b/solution.py
@@ -64,12 +64,20 @@
     count_y = lax.axis_size("sy")
     bits_x = count_x.bit_length() - 1
     bits_y = count_y.bit_length() - 1
-    grouped = lax.all_to_all(
-        current.reshape(2, count_x, rows_dev // count_x, width),
-        "sx",
-        split_axis=1,
-        concat_axis=1,
-        tiled=True,
+    grouped = jnp.concatenate(
+        lax.all_to_all(
+            jnp.stack(
+                jnp.split(
+                    current.reshape(2, count_x, rows_dev // count_x, width),
+                    lax.axis_size("sx"),
+                    axis=1,
+                )
+            ),
+            "sx",
+            0,
+            0,
+        ),
+        axis=1,
     )
     for bit_pos in range(bits_x):
         grouped = local_section(grouped, gates[bit_pos], 1, bit_pos)

time: 158 us -> 168 us (1.063)
  local copies, waits for them, and re-layouts: 15.1 us -> 24.9 us
    unnamed x59 -> x54, local copies, waits for them, and re-layouts: 5.51 us -> 16.1 us
where the time goes in v1:
time: 168 us; the launch traced here: 167 us
  blocking collectives  67.9 us (40%)
  waiting for transfers between devices  45 us (27%)
  local copies, waits for them, and re-layouts  24.9 us (15%)
  starting transfers between devices  14.3 us (9%)
  matrix products  8.45 us (5%)
  other arithmetic  6.08 us (4%)
    all_gather x1, blocking collectives, local(): return lax.all_gather(closed, ('sx', 'sy'), axis=1, tiled=True)  38.6 us
    all_to_all x1, blocking collectives, local(): lax.all_to_all(grouped, 'sx', split_axis=1, concat_axis=1, tiled=True)  29.3 us
    all_to_all x1, waiting for transfers between devices, local(): lax.all_to_all(jnp.stack(jnp.split(current.reshape(2, count_x, rows_dev /...  18.2 us
    unnamed x54, local copies, waits for them, and re-layouts  16.1 us
    all_to_all x1, waiting for transfers between devices, local(): lax.all_to_all(grouped, 'sy', split_axis=1, concat_axis=1, tiled=True)  14.2 us
    all_to_all x1, waiting for transfers between devices, local(): lax.all_to_all(current.reshape(2, count_y, rows_dev // count_y, width), '...  12.6 us
    all_to_all x1, starting transfers between devices, local(): lax.all_to_all(jnp.stack(jnp.split(current.reshape(2, count_x, rows_dev /...  7.31 us
    dot_general x10, matrix products, combine(): jnp.dot(joined, matrix, preferred_element_type=jnp.float32)  7.08 us
  transfers between devices with their start and end apart: 3, of which 3 were waited for; matrix products, arithmetic and copies ran while one was open for 6% of the time, Pallas kernels for 0%

profile of v1, /device:TPU:0, one launch (start us, length us, event | category | flops | bytes accessed | tf_op | source)
XLA Modules:
  0.0 167.2 jit_solution(9072420165900422877)
XLA Ops:
  0.0 1.6 fusion.149
  1.6 1.6 fusion.148
  3.1 1.6 fusion.147
  4.7 1.6 fusion.146
  6.3 1.6 fusion.145
  7.8 1.6 fusion.144
  9.4 1.6 fusion.143
  11.0 1.6 fusion.142
  12.5 7.3 %all-to-all-start = ((bf16[8,2,1,128,256]{4,3,1,2,0:T(8,128)(2,1)}), bf16[8,2,1,128,256]{4,3,1,2,0:T(8,128)(2,1)S(1)}, u32[]{:S(2)}, u32[]{:S(2)}) async-start(bf16[8,2,1,128,256]{4,3,1,2,0:T(8,128)(2,1)} %fusion.142), calls=%async_computation | async-start | bytes 2097152 | tf_op jit(solution)/shard_map/all_to_all | solution.py:68
  19.8 1.9 %slice_bitcast_fusion = (bf16[2,2,256,256]{3,2,1,0:T(8,128)(2,1)S(1)}, bf16[2,2,256,256]{3,2,1,0:T(8,128)(2,1)S(1)}, bf16[2,2,256,256]{3,2,1,0:T(8,128)(2,1)S(1)...) fusion(bf16[5,2,2,256,256]{4,3,2,1,0:T(8,128)(2,1)} %param.5), kind=kLoop, calls=%fused_computation.162 | loop fusion | bytes 5242880 | tf_op jit(solution)/shard_map/squeeze | solution.py:95
  23.2 0.9 maximum_multiply_fusion
  24.9 0.9 maximum_multiply_fusion.2
  26.5 0.9 maximum_multiply_fusion.4
  27.4 18.2 %all-to-all-done = bf16[8,2,1,128,256]{4,3,1,2,0:T(8,128)(2,1)S(1)} async-done(((bf16[8,2,1,128,256]{4,3,1,2,0:T(8,128)(2,1)}), bf16[8,2,1,128,256]{4,3,1,2,0:T(8,128)(2,1)S(1)}, u32[]{:S(2)}, u32[]{:S(2)}) %all-to-all-start) | async-done | bytes 1048608 | tf_op jit(solution)/shard_map/all_to_all | solution.py:68
  45.7 0.8 copy-done.17
  54.5 29.3 %all_to_all.20 = bf16[2,8,128,256]{3,2,0,1:T(8,128)(2,1)S(1)} all-to-all(bf16[2,8,128,256]{3,2,0,1:T(8,128)(2,1)S(1)} %copy.83), channel_id=1, replica_groups=mesh['sx'=8,'sy'=4] {'sx'}, dimensions={1} | all-to-all | bytes 2097152 | tf_op jit(solution)/shard_map/all_to_all | solution.py:84
  83.9 1.1 copy.85
  85.0 3.5 %all-to-all-start.2 = ((bf16[2,4,256,256]{3,2,0,1:T(8,128)(2,1)}), bf16[2,4,256,256]{3,2,0,1:T(8,128)(2,1)S(1)}, u32[]{:S(2)}, u32[]{:S(2)}) async-start(bf16[2,4,256,256]{3,2,0,1:T(8,128)(2,1)} %copy.85), calls=%async_computation.2 | async-start | bytes 2097152 | tf_op jit(solution)/shard_map/all_to_all | solution.py:87
  89.3 0.9 maximum_multiply_fusion.6
  90.3 12.6 %all-to-all-done.2 = bf16[2,4,256,256]{3,2,0,1:T(8,128)(2,1)S(1)} async-done(((bf16[2,4,256,256]{3,2,0,1:T(8,128)(2,1)}), bf16[2,4,256,256]{3,2,0,1:T(8,128)(2,1)S(1)}, u32[]{:S(2)}, u32[]{:S(2)}) %all-to-all-start.2) | async-done | bytes 1048608 | tf_op jit(solution)/shard_map/all_to_all | solution.py:87
  107.6 1.1 copy.92
  108.6 3.5 %all-to-all-start.3 = ((bf16[2,4,256,256]{3,2,0,1:T(8,128)(2,1)}), bf16[2,4,256,256]{3,2,0,1:T(8,128)(2,1)S(1)}, u32[]{:S(2)}, u32[]{:S(2)}) async-start(bf16[2,4,256,256]{3,2,0,1:T(8,128)(2,1)} %copy.92), calls=%async_computation.3 | async-start | bytes 2097152 | tf_op jit(solution)/shard_map/all_to_all | solution.py:96
  112.4 14.2 %all-to-all-done.3 = bf16[2,4,256,256]{3,2,0,1:T(8,128)(2,1)S(1)} async-done(((bf16[2,4,256,256]{3,2,0,1:T(8,128)(2,1)}), bf16[2,4,256,256]{3,2,0,1:T(8,128)(2,1)S(1)}, u32[]{:S(2)}, u32[]{:S(2)}) %all-to-all-start.3) | async-done | bytes 1048608 | tf_op jit(solution)/shard_map/all_to_all | solution.py:96
  128.1 38.6 %all_gather.3 = f32[2,4096]{1,0:T(2,128)S(1)} all-gather(f32[2,128]{1,0:T(2,128)S(1)} %pad_maximum_fusion.3), channel_id=1, replica_groups=mesh['sx'=8,'sy'=4] {'sx','sy'}, dimensions={1}, use_global_device_ids=true | all-gather | bytes 33792 | tf_op jit(solution)/shard_map/all_gather | solution.py:100
  (100 shorter events, 18.6 us)
Async XLA Ops:
  12.5 33.1 %all-to-all-start = ((bf16[8,2,1,128,256]{4,3,1,2,0:T(8,128)(2,1)}), bf16[8,2,1,128,256]{4,3,1,2,0:T(8,128)(2,1)S(1)}, u32[]{:S(2)}, u32[]{:S(2)}) async-start(bf16[8,2,1,128,256]{4,3,1,2,0:T(8,128)(2,1)} %fusion.142), calls=%async_computation | async-start | bytes 2097152 | tf_op jit(solution)/shard_map/all_to_all | solution.py:68
  45.6 0.9 copy-start.17
  45.6 1.0 copy-start.18
  45.6 1.0 copy-start.19
  46.6 0.9 copy-start.5
  46.6 1.0 copy-start.6
  48.5 0.9 copy-start.11
  48.5 1.0 copy-start.12
  48.5 1.0 copy-start.16
  49.6 0.9 copy-start.3
  49.6 1.0 copy-start.4
  51.5 0.9 copy-start.10
  51.5 1.0 copy-start.15
  52.4 0.9 copy-start.1
  52.4 1.0 copy-start.2
  85.0 17.9 %all-to-all-start.2 = ((bf16[2,4,256,256]{3,2,0,1:T(8,128)(2,1)}), bf16[2,4,256,256]{3,2,0,1:T(8,128)(2,1)S(1)}, u32[]{:S(2)}, u32[]{:S(2)}) async-start(bf16[2,4,256,256]{3,2,0,1:T(8,128)(2,1)} %copy.85), calls=%async_computation.2 | async-start | bytes 2097152 | tf_op jit(solution)/shard_map/all_to_all | solution.py:87
  89.3 13.7 %copy-start.14 = (bf16[256,256]{1,0:T(8,128)(2,1)S(1)}, bf16[256,256]{1,0:T(8,128)(2,1)}, u32[]{:S(2)}) copy-start(bf16[256,256]{1,0:T(8,128)(2,1)} %get-tuple-element.107) | copy-start | bytes 393220
  103.0 1.0 copy-start.7
  103.0 1.0 copy-start.8
  104.9 0.9 copy-start.13
  107.6 4.6 %copy-start.9 = (f32[2,128,256]{2,1,0:T(8,128)S(1)}, f32[2,128,256]{2,1,0:T(8,128)}, u32[]{:S(2)}) copy-start(f32[2,128,256]{2,1,0:T(8,128)} %param.7) | copy-start | bytes 786436
  108.6 17.9 %all-to-all-start.3 = ((bf16[2,4,256,256]{3,2,0,1:T(8,128)(2,1)}), bf16[2,4,256,256]{3,2,0,1:T(8,128)(2,1)S(1)}, u32[]{:S(2)}, u32[]{:S(2)}) async-start(bf16[2,4,256,256]{3,2,0,1:T(8,128)(2,1)} %copy.92), calls=%async_computation.3 | async-start | bytes 2097152 | tf_op jit(solution)/shard_map/all_to_all | solution.py:96
  112.2 14.5 %copy-start = (bf16[2,128,1024]{2,1,0:T(8,128)(2,1)S(1)}, bf16[2,128,1024]{2,1,0:T(8,128)(2,1)}, u32[]{:S(2)}) copy-start(bf16[2,128,1024]{2,1,0:T(8,128)(2,1)} %param.6) | copy-start | bytes 1572868
